TPU v7x, 128 devices: a whole 4x4x4 slice. The times are simulated.
128 devices in a mesh: dp: 32 (over y, z, x_hi), mp: 4 (over x_lo, core).
Axes of the slice: x: 4 (x_hi: 2, x_lo: 2; x = x_hi * 2 + x_lo), y: 4, z: 4, core: 2. Of those that a mesh axis runs over, the one named last changes fastest.
Arguments:
- slow_weights: float32 [1, 3584, 1024], P(None, None, 'mp'), may hold values from -6 to 6
- fast_weights: bfloat16 [32, 1, 3584, 1024], P('dp', None, None, 'mp'), may hold values from -64 to 64
- momentum: float32 [1, 3584, 1024], P(None, None, 'mp'), may hold values from -1.2 to 1.2
Outputs:
- slow_next: float32 [1, 3584, 1024], P(None, None, 'mp')
- momentum_next: float32 [1, 3584, 1024], P(None, None, 'mp')
- fast_next: bfloat16 [32, 1, 3584, 1024], P('dp', None, None, 'mp')
All inputs are finite; a program needn't handle non-finite values.
Results may differ from a plain program's by a relative error of at most 0.001.
Values sent between devices are 32-bit elements; how exact they have to be, the bound alone decides.
A program may use at most 64 MiB of HBM per device.

v0:
```python
import math

import jax
import jax.numpy as jnp
from jax import lax
from jax.sharding import PartitionSpec as P

MOMENTUM_RATE = 0.9
OUTER_RATE = 0.7
CLIP_LEVEL = 0.2
EPSILON = 1e-06


def split_up(x, dim, size):
    before, after = (x.shape[:dim], x.shape[dim + 1 :])
    return jnp.moveaxis(x.reshape(*before, size, -1, *after), dim, 0)


def sent_and_summed(x, axis, dim):
    parts = split_up(x, dim, lax.axis_size(axis))
    arrived = lax.all_to_all(parts, axis, split_axis=0, concat_axis=0, tiled=True)
    return arrived.sum(axis=0)


def padded_to(lines, size):
    spare = -lines.shape[0] % size
    if not spare:
        return lines
    return jnp.concatenate([lines, jnp.zeros((spare, *lines.shape[1:]), lines.dtype)])


def joined_along(parts, dim):
    lengths = list(parts.shape[1:])
    lengths[dim] *= parts.shape[0]
    return jnp.moveaxis(parts, 0, dim).reshape(lengths)


def from_everyone(x, axis):
    size = lax.axis_size(axis)
    return lax.all_to_all(jnp.broadcast_to(x[None], (size, *x.shape)), axis, 0, 0, tiled=True)


def gathered_copies(x, axis, dim):
    return joined_along(from_everyone(x, axis), dim)


def nested_sum(x, axes):
    lines = x.reshape(-1, x.shape[-1])
    own = sent_and_summed(padded_to(lines, lax.axis_size(axes)), axes, 0)
    whole = gathered_copies(own, axes, 0)
    return whole[: len(lines)].reshape(x.shape)


def taken_together(x, axis):
    return from_everyone(x, axis).sum(axis=0)


def apply_update(slow_part, momentum_part, pseudo, squares, max_norm):
    factor = jnp.minimum(1.0, max_norm / (jnp.sqrt(squares) + EPSILON))
    gradient = factor * pseudo
    momentum_next = MOMENTUM_RATE * momentum_part + gradient
    slow_next = slow_part - OUTER_RATE * (gradient + MOMENTUM_RATE * momentum_next)
    return (slow_next, momentum_next)


def body(slow_weights, fast_weights, momentum):
    difference = slow_weights - fast_weights[0].astype(jnp.float32)
    replicas = lax.axis_size("dp")
    entries = (
        slow_weights.shape[0] * slow_weights.shape[1] * slow_weights.shape[2] * lax.axis_size("mp")
    )
    max_norm = CLIP_LEVEL * math.sqrt(entries)
    pseudo = nested_sum(difference, "dp") / replicas
    squares = taken_together(jnp.sum(pseudo * pseudo), "mp")
    slow_next, momentum_next = apply_update(slow_weights, momentum, pseudo, squares, max_norm)
    fast_next = slow_next.astype(jnp.bfloat16)[None]
    return (slow_next, momentum_next, fast_next)


def solution(mesh):
    in_specs = (P(None, None, "mp"), P("dp", None, None, "mp"), P(None, None, "mp"))
    out_specs = (P(None, None, "mp"), P(None, None, "mp"), P("dp", None, None, "mp"))
    return jax.shard_map(body, mesh=mesh, in_specs=in_specs, out_specs=out_specs, check_vma=False)
```

profile of v0, /device:TPU:0, one launch (start us, length us, event | category | flops | bytes accessed | tf_op | source)
XLA Modules:
  0.0 134.3 jit_solution(17695536789648378248)
XLA Ops:
  0.6 3.0 %convert_subtract_fusion = f32[1,3584,256]{2,1,0:T(8,128)S(1)} fusion(f32[1,3584,256]{2,1,0:T(8,128)} %param.3, bf16[1,1,3584,256]{3,2,1,0:T(8,128)(2,1)} %param.4), kind=kLoop, calls=%fused_computation | loop fusion | flops 1835008 | bytes 9175040 | tf_op jit(solution)/shard_map/sub | solution.py:67
  3.6 58.3 %all_to_all.16 = f32[32,112,256]{2,1,0:T(8,128)} all-to-all(f32[32,112,256]{2,1,0:T(8,128)S(1)} %bitcast.16), channel_id=1, replica_groups=mesh['dp'=32,'mp'=4] {'dp'}, dimensions={0} | all-to-all | bytes 7340032 | tf_op jit(solution)/shard_map/all_to_all | solution.py:21
  61.9 2.3 %reduce_sum.27 = f32[112,256]{1,0:T(8,128)S(1)} reduce(f32[32,112,256]{2,1,0:T(8,128)} %all_to_all.16, f32[]{:T(128)} %constant.1.clone.1), dimensions={0}, to_apply=%region_0.0 | reduce | flops 888832 | bytes 3784708 | tf_op jit(solution)/shard_map/reduce_sum | solution.py:22
  64.2 0.4 broadcast_in_dim.6
  64.6 49.3 %all_to_all.17 = f32[32,112,256]{2,1,0:T(8,128)S(1)} all-to-all(f32[32,112,256]{2,1,0:T(8,128)S(1)} %broadcast_in_dim.6), channel_id=1, replica_groups=mesh['dp'=32,'mp'=4] {'dp'}, dimensions={0} | all-to-all | bytes 7340032 | tf_op jit(solution)/shard_map/all_to_all | solution.py:40
  113.9 0.0 copy-start
  113.9 1.8 %copy-done = f32[32,112,256]{2,1,0:T(8,128)} copy-done((f32[32,112,256]{2,1,0:T(8,128)}, f32[32,112,256]{2,1,0:T(8,128)S(1)}, u32[]{:S(2)}) %copy-start) | copy-done | bytes 3670040
  115.7 1.5 %multiply_reduce_fusion = f32[]{:T(128)} fusion(f32[32,112,256]{2,1,0:T(8,128)S(1)} %all_to_all.17), kind=kLoop, calls=%fused_computation.5 | loop fusion | flops 2752511 | bytes 3670020 | tf_op jit(solution)/shard_map/reduce_sum | solution.py:74
  117.3 0.6 broadcast_in_dim.7
  117.9 6.2 %all_to_all.18 = f32[4,1,1]{2,1,0:T(1,128)S(1)} all-to-all(f32[4,1,1]{2,1,0:T(1,128)S(1)} %broadcast_in_dim.7), channel_id=1, replica_groups=mesh['dp'=32,'mp'=4] {'mp'}, dimensions={0} | all-to-all | bytes 32 | tf_op jit(solution)/shard_map/all_to_all | solution.py:40
  124.1 0.6 reduce_sum.29
  125.5 0.0 copy-start.1
  125.5 0.0 copy-start.2
  125.5 2.4 %broadcast_multiply_fusion = f32[32,112,256]{2,1,0:T(8,128)S(1)} fusion(f32[32,112,256]{2,1,0:T(8,128)} %copy-done, f32[]{:T(128)S(6)} %mul.38), kind=kLoop, calls=%fused_computation.7 | loop fusion | flops 917504 | bytes 7340036 | tf_op jit(solution)/shard_map/mul | solution.py:60
  128.0 0.7 copy-done.1
  128.6 1.1 copy-done.2
  129.7 4.6 %convert_bitcast_fusion = (bf16[1,1,3584,256]{3,2,1,0:T(8,128)(2,1)}, f32[1,3584,256]{2,1,0:T(8,128)}, f32[1,3584,256]{2,1,0:T(8,128)}) fusion(f32[1,3584,256]{2,1,0:T(8,128)S(1)} %copy-done.1, f32[1,3584,256]{2,1,0:T(8,128)S(1)} %copy-done.2, f32[1,3584,256]{2,1,0:T(8,128)S(1)} %bitcast.15), kind=kLoop, calls=%fused_computation.6 | loop fusion | flops 6422528 | bytes 20185088 | tf_op jit(solution)/shard_map/broadcast_in_dim | solution.py:76
Async XLA Ops:
  113.9 1.8 %copy-start = (f32[32,112,256]{2,1,0:T(8,128)}, f32[32,112,256]{2,1,0:T(8,128)S(1)}, u32[]{:S(2)}) copy-start(f32[32,112,256]{2,1,0:T(8,128)S(1)} %all_to_all.17) | copy-start | bytes 11010052
  125.5 3.1 %copy-start.1 = (f32[1,3584,256]{2,1,0:T(8,128)S(1)}, f32[1,3584,256]{2,1,0:T(8,128)}, u32[]{:S(2)}) copy-start(f32[1,3584,256]{2,1,0:T(8,128)} %param.3) | copy-start | bytes 11010052
  125.5 4.3 %copy-start.2 = (f32[1,3584,256]{2,1,0:T(8,128)S(1)}, f32[1,3584,256]{2,1,0:T(8,128)}, u32[]{:S(2)}) copy-start(f32[1,3584,256]{2,1,0:T(8,128)} %param.5) | copy-start | bytes 11010052
where the time goes:
time: 135 us; the launch traced here: 134 us
  blocking collectives  114 us (84%)
  other arithmetic  14.4 us (11%)
  local copies, waits for them, and re-layouts  4.69 us (3%)
  between operations  1.41 us (1%)
    all_to_all x1, blocking collectives, sent_and_summed(): lax.all_to_all(parts, axis, split_axis=0, concat_axis=0, tiled=True)  58.3 us
    all_to_all x2, blocking collectives, from_everyone(): lax.all_to_all(jnp.broadcast_to(x[None], (size, *x.shape)), axis, 0, 0, t...  55.5 us
    broadcast_in_dim x1, other arithmetic, body(): fast_next = slow_next.astype(jnp.bfloat16)[None]  4.58 us
    unnamed x6, local copies, waits for them, and re-layouts  3.64 us
    sub x1, other arithmetic, body(): difference = slow_weights - fast_weights[0].astype(jnp.float32)  2.97 us

commit v1 on v0

v1 whole, which is shorter than its diff:
```python
import math

import jax
import jax.numpy as jnp
from jax import lax
from jax.experimental import pallas as pl
from jax.experimental.pallas import tpu as pltpu
from jax.sharding import PartitionSpec as P

MOMENTUM_RATE = 0.9
OUTER_RATE = 0.7
CLIP_LEVEL = 0.2
EPSILON = 1e-06

MESH = pl.DeviceIdType.MESH
UNIT = 256
CHUNKS = (
    ("yzx", 256), ("zyx", 256), ("xyz", 256),
    ("yzx", 256), ("zyx", 256), ("xzy", 256),
    ("yzx", 256), ("zyx", 256), ("xyz", 256),
    ("yzx", 256), ("zyx", 256), ("xzy", 256),
    ("yzx", 256), ("zyx", 256),
)
RATE = 46.6e3
LATENCY = {1: 2.0, 2: 2.7}


class Event:
    def __init__(self, name, waits, sends, cost, run):
        self.name, self.waits, self.sends, self.cost, self.run = name, waits, sends, cost, run


def in_order(events):
    arrival, free, now, left, done = {}, {}, 0.0, list(events), []
    while left:
        best = None
        for event in left:
            if all(w in arrival for w in event.waits):
                ready = max([arrival[w] for w in event.waits], default=0.0)
                if best is None or ready < best[0]:
                    best = (ready, event)
        ready, event = best
        left.remove(event)
        done.append(event)
        now = max(now, ready) + event.cost
        for key, links, size, hops in event.sends:
            start = max([now] + [free.get(link, 0.0) for link in links])
            for link in links:
                free[link] = start + size / RATE
            arrival[key] = start + size / RATE + LATENCY[hops]
    return done, now


class Plan:
    def __init__(self, here, send_sems, recv_sems):
        self.here, self.send_sems, self.recv_sems = here, send_sems, recv_sems
        self.ids, self.out, self.shape = {}, [], {}

    def index(self, key):
        return self.ids.setdefault(key, len(self.ids))

    def send(self, key, src, dst, device):
        i = self.index(key)
        copy = pltpu.make_async_remote_copy(
            src_ref=src,
            dst_ref=dst,
            send_sem=self.send_sems.at[i],
            recv_sem=self.recv_sems.at[i],
            device_id=device,
            device_id_type=MESH,
        )
        copy.start()
        self.out.append(copy)
        self.shape[key] = copy

    def wait(self, key):
        self.shape[key].wait_recv()


def place():
    dp, mp = lax.axis_index("dp"), lax.axis_index("mp")
    return {"y": dp // 8, "z": lax.rem(dp // 2, 4), "x": lax.rem(dp, 2)}, dp, mp


def moved(at, axis, by):
    to = dict(at)
    to[axis] = lax.rem(at[axis] + by, 2 if axis == "x" else 4)
    return {"dp": (to["y"] * 4 + to["z"]) * 2 + to["x"]}


def rows(start, size):
    return pl.ds(pl.multiple_of(start, 8), size)


def ring_pos(at, axis, by):
    return lax.rem(at[axis] + by, 4)


def chunk_events(tag, order, base, size, at, plan, refs, events):
    diff, out, recv, squares, slot = refs["diff"], refs["out"], refs["recv"], refs["squares"], refs["slot"]
    alloc = refs["alloc"]

    def key(*what):
        return (tag,) + what

    def two(axis):
        return (axis + "+", axis + "-")

    def byte(n):
        return n * 1024

    starts, sizes = [base], [size]
    for axis in order:
        n = 2 if axis == "x" else 4
        sizes.append(sizes[-1] // n)
        starts.append(starts[-1] + at[axis] * sizes[-1])

    def emit(name, waits, sends, cost, run):
        events.append(Event(key(name), waits, sends, cost, run))

    pending = []

    def add_into(start, n, keys):
        def run():
            for k in keys:
                plan.wait(k)
            total = diff[rows(start, n)]
            for k in keys:
                total = total + recv[pl.ds(alloc[k], n)]
            diff[rows(start, n)] = total

        return run

    prepare, waits = refs["load"](base, size), []
    cost = 0.25
    big = True
    for level, axis in enumerate(order):
        start, part = starts[level], sizes[level + 1]
        if axis == "x":
            k = key("rs", level)
            alloc[k] = slot(part)

            def run(prepare=prepare, k=k, start=start, part=part):
                prepare()
                src = rows(start + (1 - at["x"]) * part, part)
                plan.send(k, diff.at[src], recv.at[pl.ds(alloc[k], part)], moved(at, "x", 1))

            emit(("rs", level), waits, [(k, two("x"), byte(part), 2)], cost, run)
            prepare, waits = add_into(starts[level + 1], part, [k]), [k]
        elif big:
            big = False
            half = part // 2
            for k in ("far+", "far-", "in+", "in-", "dep+", "dep-"):
                alloc[key(k)] = slot(half)

            def run(prepare=prepare, axis=axis, start=start, part=part, half=half):
                prepare()
                right, left = moved(at, axis, 1), moved(at, axis, 3)
                p1, p2, p3 = (start + ring_pos(at, axis, i) * part for i in (1, 2, 3))
                for k, src, device in (
                    ("far+", p2, right),
                    ("far-", p2 + half, left),
                    ("in+", p1 + half, right),
                    ("in-", p3, left),
                ):
                    plan.send(key(k), diff.at[rows(src, half)], recv.at[pl.ds(alloc[key(k)], half)], device)

            emit(
                ("rs", level),
                waits,
                [(key(k), (axis + k[-1],), byte(half), 1) for k in ("far+", "far-", "in+", "in-")],
                cost,
                run,
            )
            for sign, by, off in (("+", 1, 0), ("-", 3, half)):

                def run(sign=sign, by=by, off=off, axis=axis, start=start, part=part, half=half):
                    src = start + ring_pos(at, axis, by) * part + off
                    add_into(src, half, [key("far" + sign)])()
                    k = key("dep" + sign)
                    plan.send(
                        k, diff.at[rows(src, half)], recv.at[pl.ds(alloc[k], half)], moved(at, axis, by)
                    )

                emit(
                    "dep" + sign,
                    [key("far" + sign)],
                    [(key("dep" + sign), (axis + sign,), byte(half), 1)],
                    0.05,
                    run,
                )
            first = add_into(starts[level + 1], half, [key("dep+"), key("in-")])
            second = add_into(starts[level + 1] + half, half, [key("in+"), key("dep-")])

            def prepare(first=first, second=second):
                first()
                second()

            waits = [key(k) for k in ("dep+", "in-", "in+", "dep-")]
        else:
            for by in (1, 2, 3):
                alloc[key("rs", level, by)] = slot(part)

            def run(prepare=prepare, axis=axis, start=start, part=part, level=level):
                prepare()
                for by in (1, 3, 2):
                    k = key("rs", level, by)
                    src = start + ring_pos(at, axis, by) * part
                    plan.send(k, diff.at[rows(src, part)], recv.at[pl.ds(alloc[k], part)], moved(at, axis, by))

            emit(
                ("rs", level),
                waits,
                [
                    (key("rs", level, 1), (axis + "+",), byte(part), 1),
                    (key("rs", level, 3), (axis + "-",), byte(part), 1),
                    (key("rs", level, 2), two(axis), byte(part), 2),
                ],
                cost,
                run,
            )
            keys = [key("rs", level, by) for by in (1, 2, 3)]
            prepare, waits = add_into(starts[level + 1], part, keys), keys
        cost = 0.1

    shard, n = starts[3], sizes[3]

    def settle(prepare=prepare):
        prepare()
        total = diff[rows(shard, n)]
        out[rows(shard, n)] = total
        square = total * total
        square = square[:, :128] + square[:, 128:]
        squares[...] += square.reshape(n // 8, 8, 128).sum(axis=0)

    prepare = settle
    refs["settled"].append(waits)
    for level in (2, 1, 0):
        axis = order[level]
        start, part = starts[level + 1], sizes[level + 1]
        if axis == "x":
            k = key("ag", level)

            def run(prepare=prepare, k=k, start=start, part=part):
                prepare()
                plan.send(k, out.at[rows(start, part)], out.at[rows(start, part)], moved(at, "x", 1))

            emit(("ag", level), waits, [(k, two("x"), byte(part), 2)], cost, run)
            waits = [k]
        elif level == (0 if order[0] != "x" else 1):
            half = part // 2

            def run(prepare=prepare, axis=axis, start=start, half=half):
                prepare()
                right, left = moved(at, axis, 1), moved(at, axis, 3)
                for k, src, device in (
                    ("on+", start, right),
                    ("on-", start + half, left),
                    ("end+", start + half, right),
                    ("end-", start, left),
                ):
                    plan.send(key(k), out.at[rows(src, half)], out.at[rows(src, half)], device)

            emit(
                ("ag", level),
                waits,
                [(key(k), (axis + k[-1],), byte(half), 1) for k in ("on+", "on-", "end+", "end-")],
                cost,
                run,
            )
            for sign, by, off in (("+", 1, 0), ("-", 3, half)):

                def run(sign=sign, by=by, off=off, axis=axis, level=level, part=part, half=half):
                    plan.wait(key("on" + sign))
                    src = starts[level] + ring_pos(at, axis, 4 - by) * part + off
                    k = key("last" + sign)
                    plan.send(k, out.at[rows(src, half)], out.at[rows(src, half)], moved(at, axis, by))

                emit(
                    "last" + sign,
                    [key("on" + sign)],
                    [(key("last" + sign), (axis + sign,), byte(half), 1)],
                    0.02,
                    run,
                )
            waits = [key(k) for k in ("end+", "end-", "last+", "last-")]
        else:

            def run(prepare=prepare, axis=axis, start=start, part=part, level=level):
                prepare()
                for by in (1, 3, 2):
                    k = key("ag", level, by)
                    plan.send(k, out.at[rows(start, part)], out.at[rows(start, part)], moved(at, axis, by))

            emit(
                ("ag", level),
                waits,
                [
                    (key("ag", level, 1), (axis + "+",), byte(part), 1),
                    (key("ag", level, 3), (axis + "-",), byte(part), 1),
                    (key("ag", level, 2), two(axis), byte(part), 2),
                ],
                cost,
                run,
            )
            waits = [key("ag", level, by) for by in (1, 2, 3)]
        cost = 0.02

        def prepare(waits=waits):
            for k in waits:
                plan.wait(k)

    emit("end", waits, [], 0.02, prepare)


def norm_events(at, mp, plan, refs, events):
    squares, parts = refs["squares"], refs["parts"]
    waits = [k for keys in refs["settled"] for k in keys]
    waits = list(dict.fromkeys(waits))
    slots = [0]

    def round_of(name, peers, waits, before):
        keys = [("norm", name, i) for i in range(len(peers))]
        base = slots[0]
        slots[0] += len(peers)

        def run():
            before()
            for i, (device, links, hops) in enumerate(peers):
                plan.send(keys[i], squares.at[name], parts.at[base + i], device)

        def after():
            total = squares[name]
            for i, k in enumerate(keys):
                plan.wait(k)
                total = total + parts[base + i]
            squares[name + 1] = total

        sends = [(k, links, 4096, hops) for k, (_, links, hops) in zip(keys, peers)]
        events.append(Event(("norm", name), waits, sends, 0.05, run))
        return keys, after

    def line(axis):
        return [
            (moved(at, axis, 1), (axis + "+",), 1),
            (moved(at, axis, 3), (axis + "-",), 1),
            (moved(at, axis, 2), (axis + "+", axis + "-"), 2),
        ]

    def nothing():
        pass

    keys, after = round_of(0, line("y"), waits, nothing)
    keys, after = round_of(1, line("z"), keys, after)
    peers = []
    for flip in (0, 1):
        for by in range(4):
            if flip or by:
                device = dict(moved(at, "x", flip), mp=lax.rem(mp + by, 4))
                peers.append((device, ("x+", "x-"), 2))
    keys, after = round_of(2, peers, keys, after)
    events.append(Event(("norm", "end"), keys, [], 0.1, after))
    return peers


def kernel(max_norm, count, slow, fast, out, factor, slow_in, fast_in, diff, recv, squares, parts, load_sems, send_sems, recv_sems):
    at, dp, mp = place()
    loads = []
    base = 0
    for i, (_, size) in enumerate(CHUNKS):
        part = pl.ds(base, size)
        for j, (src, dst) in enumerate(((slow, slow_in), (fast, fast_in))):
            copy = pltpu.make_async_copy(src.at[part], dst.at[part], load_sems.at[i, j])
            copy.start()
            loads.append(copy)
        base += size
    squares[...] = jnp.zeros_like(squares)

    plan = Plan(at, send_sems, recv_sems)
    taken = [0]

    def slot(n):
        taken[0] += n
        return taken[0] - n

    def load(base, size):
        index = load.calls
        load.calls += 1

        def run():
            loads[2 * index].wait()
            loads[2 * index + 1].wait()
            part = pl.ds(base, size)
            diff[part] = slow_in[part] - fast_in[part].astype(jnp.float32)

        return run

    load.calls = 0
    refs = {
        "diff": diff, "out": out, "recv": recv, "squares": squares.at[0], "slot": slot,
        "alloc": {}, "load": load, "settled": [],
    }
    events = []
    base = 0
    for i, (order, size) in enumerate(CHUNKS):
        chunk_events(i, order, base, size, at, plan, refs, events)
        base += size
    refs["squares"], refs["parts"] = squares, parts
    peers = norm_events(at, mp, plan, refs, events)
    events, _ = in_order(events)

    barrier = pltpu.get_barrier_semaphore()
    friends = [moved(at, axis, by) for axis in "yz" for by in (1, 2, 3)] + [p[0] for p in peers]
    for device in friends:
        pl.semaphore_signal(barrier, inc=1, device_id=device, device_id_type=MESH)
    pl.semaphore_wait(barrier, len(friends))

    for event in events:
        event.run()
    total = jnp.sum(squares[3], axis=(0, 1), keepdims=True) / (count * count)
    scale = jnp.minimum(1.0, max_norm / (jnp.sqrt(total) + EPSILON)) / count
    factor[...] = jnp.broadcast_to(scale, factor.shape)
    for copy in plan.out:
        copy.wait_send()


def summed(slow, fast, max_norm, count):
    n = slow.shape[0]
    any_space = pl.BlockSpec(memory_space=pl.ANY)
    vmem = pl.BlockSpec(memory_space=pltpu.VMEM)
    f32 = jnp.float32
    return pl.pallas_call(
        lambda *refs: kernel(max_norm, count, *refs),
        out_shape=(jax.ShapeDtypeStruct((n, slow.shape[1]), f32), jax.ShapeDtypeStruct((8, 128), f32)),
        in_specs=[any_space, any_space],
        out_specs=(vmem, vmem),
        scratch_shapes=[
            pltpu.VMEM(slow.shape, f32),
            pltpu.VMEM(fast.shape, fast.dtype),
            pltpu.VMEM(slow.shape, f32),
            pltpu.VMEM((5000, slow.shape[1]), f32),
            pltpu.VMEM((4, 8, 128), f32),
            pltpu.VMEM((13, 8, 128), f32),
            pltpu.SemaphoreType.DMA((len(CHUNKS), 2)),
            pltpu.SemaphoreType.DMA((400,)),
            pltpu.SemaphoreType.DMA((400,)),
        ],
        compiler_params=pltpu.CompilerParams(
            collective_id=0, has_side_effects=True, vmem_limit_bytes=40 * 1024 * 1024
        ),
        name="summed",
    )(slow, fast)


def body(slow_weights, fast_weights, momentum):
    replicas = lax.axis_size("dp")
    entries = slow_weights.shape[0] * slow_weights.shape[1] * slow_weights.shape[2] * lax.axis_size("mp")
    max_norm = CLIP_LEVEL * math.sqrt(entries)
    total, factor = summed(slow_weights[0], fast_weights[0, 0], max_norm, replicas)
    gradient = factor[0, 0] * total[None]
    momentum_next = MOMENTUM_RATE * momentum + gradient
    slow_next = slow_weights - OUTER_RATE * (gradient + MOMENTUM_RATE * momentum_next)
    return (slow_next, momentum_next, slow_next.astype(jnp.bfloat16)[None])


def solution(mesh):
    in_specs = (P(None, None, "mp"), P("dp", None, None, "mp"), P(None, None, "mp"))
    out_specs = (P(None, None, "mp"), P(None, None, "mp"), P("dp", None, None, "mp"))
    return jax.shard_map(body, mesh=mesh, in_specs=in_specs, out_specs=out_specs, check_vma=False)
```

time: 135 us -> 75.3 us (0.56)
  blocking collectives: 114 us -> 0 us
  Pallas kernels: 0 us -> 63.1 us
  other arithmetic: 14.4 us -> 7.24 us
    all_to_all x3 -> x0, blocking collectives: 114 us -> none  [the longest x1 58.3 us: sent_and_summed(): lax.all_to_all(parts, axis, split_axis=0, concat_axis=0, tiled=True)]
    pallas_call x0 -> x1, Pallas kernels: none -> 63.1 us  [summed(): pl.pallas_call(lambda *refs: kernel(max_norm, count, *refs), out_shape=(j...]
    reduce_sum x3 -> x0, other arithmetic: 4.41 us -> none  [the longest x1 2.26 us: sent_and_summed(): return arrived.sum(axis=0)]
    sub x1 -> x0, other arithmetic: 2.97 us -> none  [body(): difference = slow_weights - fast_weights[0].astype(jnp.float32)]
    broadcast_in_dim x1, other arithmetic: 4.58 us -> 7.24 us  [body(): return (slow_next, momentum_next, slow_next.astype(jnp.bfloat16)[None])]
    mul x1 -> x0, other arithmetic: 2.44 us -> none  [apply_update(): gradient = factor * pseudo]
where the time goes in v1:
time: 75.3 us; the launch traced here: 75.1 us
  Pallas kernels  63.1 us (84%)
  other arithmetic  7.24 us (10%)
  local copies, waits for them, and re-layouts  4.06 us (5%)
    pallas_call x1, Pallas kernels, summed(): pl.pallas_call(lambda *refs: kernel(max_norm, count, *refs), out_shape=(j...  63.1 us
    broadcast_in_dim x1, other arithmetic, body(): return (slow_next, momentum_next, slow_next.astype(jnp.bfloat16)[None])  7.24 us
    unnamed x6, local copies, waits for them, and re-layouts  3.53 us

profile of v1, /device:TPU:0, one launch (start us, length us, event | category | flops | bytes accessed | tf_op | source)
XLA Modules:
  0.0 75.1 jit_solution(9738893164125788387)
XLA Ops:
  0.6 0.0 copy-start
  0.6 2.0 %copy-done = f32[1,3584,256]{2,1,0:T(8,128)S(1)} copy-done((f32[1,3584,256]{2,1,0:T(8,128)S(1)}, f32[1,3584,256]{2,1,0:T(8,128)}, u32[]{:S(2)}) %copy-start) | copy-done | bytes 3670040
  2.7 0.0 copy-start.2
  2.7 1.5 %copy-done.2 = bf16[1,1,3584,256]{3,2,1,0:T(8,128)(2,1)S(1)} copy-done((bf16[1,1,3584,256]{3,2,1,0:T(8,128)(2,1)S(1)}, bf16[1,1,3584,256]{3,2,1,0:T(8,128)(2,1)}, u32[]{:S(2)}) %copy-start.2) | copy-done | bytes 1835032
  4.2 0.0 copy-start.1
  4.2 63.1 %summed.1 = (f32[3584,256]{1,0:T(8,128)S(1)}, f32[8,128]{1,0:T(8,128)S(1)}) custom-call(f32[3584,256]{1,0:T(8,128)S(1)} %bitcast.14, bf16[3584,256]{1,0:T(8,128)(2,1)S(1)} %bitcast.15), custom_call_target="tpu_custom_call" | custom-call | tf_op jit(solution)/shard_map/summed/pallas_call | solution.py:432
  67.3 0.5 slice.3
  67.8 0.0 copy-done.1
  67.8 7.2 %convert_bitcast_fusion = (bf16[1,1,3584,256]{3,2,1,0:T(8,128)(2,1)}, f32[1,3584,256]{2,1,0:T(8,128)}, f32[1,3584,256]{2,1,0:T(8,128)}) fusion(f32[1,3584,256]{2,1,0:T(8,128)S(1)} %copy-done.1, f32[3584,256]{1,0:T(8,128)S(1)} %get-tuple-element.6, f32[]{:T(128)} %bitcast.2, f32[1,3584,256]{2,1,0:T(8,128)} %param.5), kind=kLoop, calls=%fused_computation.4 | loop fusion | flops 7340032 | bytes 20185092 | tf_op jit(solution)/shard_map/broadcast_in_dim | solution.py:463
Async XLA Ops:
  0.6 2.0 %copy-start = (f32[1,3584,256]{2,1,0:T(8,128)S(1)}, f32[1,3584,256]{2,1,0:T(8,128)}, u32[]{:S(2)}) copy-start(f32[1,3584,256]{2,1,0:T(8,128)} %param.3) | copy-start | bytes 11010052
  2.7 1.5 %copy-start.2 = (bf16[1,1,3584,256]{3,2,1,0:T(8,128)(2,1)S(1)}, bf16[1,1,3584,256]{3,2,1,0:T(8,128)(2,1)}, u32[]{:S(2)}) copy-start(bf16[1,1,3584,256]{3,2,1,0:T(8,128)(2,1)} %param.4) | copy-start | bytes 5505028
  4.2 63.7 %copy-start.1 = (f32[1,3584,256]{2,1,0:T(8,128)S(1)}, f32[1,3584,256]{2,1,0:T(8,128)}, u32[]{:S(2)}) copy-start(f32[1,3584,256]{2,1,0:T(8,128)} %param.3) | copy-start | bytes 11010052

commit v2 on v0

v2 whole, which is shorter than its diff:
```python
import math

import jax
import jax.numpy as jnp
from jax import lax
from jax.experimental import pallas as pl
from jax.experimental.pallas import tpu as pltpu
from jax.sharding import PartitionSpec as P

MOMENTUM_RATE = 0.9
OUTER_RATE = 0.7
CLIP_LEVEL = 0.2
EPSILON = 1e-06

MESH = pl.DeviceIdType.MESH
LENGTH = {"x": 2, "y": 4, "z": 4}
COLUMNS = 256
Y, Z = ("r:y", "d:zx"), ("r:z", "d:yx")
XY, XZ = ("d:x", "r:y", "d:z"), ("d:x", "r:z", "d:y")
CHUNKS = (
    (XY, 256, 0.0), (Y, 256, 0.0), (Z, 256, 0.0), (XZ, 256, 0.0),
    (Y, 256, 0.0), (Z, 256, 0.0), (XY, 256, 0.0),
    (Y, 256, 0.0), (Z, 256, 0.0), (XZ, 256, 0.0),
    (Y, 256, 0.0), (Z, 256, 0.0),
    (Y, 256, 0.0), (Z, 256, 0.0),
)
LOADS = (768, 1024, 896, 896)
RATE = 46.6e3
HOP = (1.6, 0.6)
ISSUE = 0.03


class Event:
    def __init__(self, waits, run, sends=(), cost=0.02, gives=None, start=0.0):
        self.waits, self.run, self.sends = waits, run, sends
        self.cost, self.gives, self.start = cost, gives, start


def in_order(events):
    arrival, free, now, left, done = {}, {}, 0.0, list(events), []
    need = {}
    for event in events:
        for key, _, _ in event.sends:
            need[key] = need.get(key, 0) + 1
    while left:
        best = None
        for event in left:
            if all(w in arrival and not need.get(w) for w in event.waits):
                ready = max([event.start] + [arrival[w] for w in event.waits])
                if best is None or max(ready, now) < max(best[0], now):
                    best = (ready, event)
        ready, event = best
        left.remove(event)
        done.append(event)
        now = max(now, ready) + event.cost
        for key, size, hops in event.sends:
            now += ISSUE
            end = now
            for axis, by in hops:
                ways = {"y": {1: "+", 3: "-", 2: "+-"}, "z": {1: "+", 3: "-", 2: "+-"}, "x": {1: "+-"}}[axis][by]
                for way in ways:
                    begin = max(now, free.get(axis + way, 0.0))
                    free[axis + way] = begin + size / RATE
                    end = max(end, begin + size / RATE)
            count = sum(2 if axis == "x" else min(by, 4 - by) for axis, by in hops)
            arrival[key] = max(arrival.get(key, 0.0), end + HOP[0] + HOP[1] * count)
            need[key] -= 1
        if event.gives is not None:
            arrival[event.gives] = now
    return done, now


def moved(at, offsets):
    to = dict(at)
    for axis, by in offsets:
        to[axis] = lax.rem(at[axis] + by, LENGTH[axis])
    return {"dp": (to["y"] * 4 + to["z"]) * 2 + to["x"]}


def others(axes):
    found = [()]
    for axis in axes:
        found = [o + ((axis, by),) for o in found for by in range(LENGTH[axis])]
    return [tuple((a, by) for a, by in o if by) for o in found if any(by for _, by in o)]


def rows(start, size):
    return pl.ds(start if isinstance(start, int) else pl.multiple_of(start, 8), size)


class Exchange:
    def __init__(self, recv_sems, send_sems, whole):
        self.recv_sems, self.send_sems, self.whole = recv_sems, send_sems, whole
        self.index, self.size = {}, {}
        self.sent = [0, 0]

    def group(self, key, size):
        self.index.setdefault(key, len(self.index))
        self.size[key] = self.size.get(key, 0) + size

    def send(self, key, src, dst, device, phase):
        pltpu.make_async_remote_copy(
            src_ref=src,
            dst_ref=dst,
            send_sem=self.send_sems.at[phase],
            recv_sem=self.recv_sems.at[self.index[key]],
            device_id=device,
            device_id_type=MESH,
        ).start()

    def wait(self, key):
        part = self.whole.at[pl.ds(0, self.size[key])]
        pltpu.make_async_copy(part, part, self.recv_sems.at[self.index[key]]).wait()

    def drain(self, phase):
        part = self.whole.at[pl.ds(0, self.sent[phase])]
        pltpu.make_async_copy(part, part, self.send_sems.at[phase]).wait()


class Sum:
    def __init__(self, at, exchange, diff, recv, total):
        self.at, self.exchange = at, exchange
        self.diff, self.recv, self.total = diff, recv, total
        self.events, self.settled, self.taken = [], [], 0

    def copy_of(self, key, size, offsets):
        return (key, size * COLUMNS * 4, offsets)

    def expect(self, key, size, phase):
        self.exchange.group(key, size)
        self.exchange.sent[phase] += size

    def slot(self, size):
        self.taken += size
        return self.taken - size

    def add_into(self, start, size, places):
        value = self.diff[rows(start, size)]
        for place in places:
            value = value + self.recv[pl.ds(place, size)]
        self.diff[rows(start, size)] = value

    def scatter(self, key, src, place, size, offsets):
        src_ref, dst_ref = self.diff.at[rows(src, size)], self.recv.at[pl.ds(place, size)]
        self.exchange.send(key, src_ref, dst_ref, moved(self.at, offsets), 0)

    def gather(self, key, start, size, offsets):
        ref = self.total.at[rows(start, size)]
        self.exchange.send(key, ref, ref, moved(self.at, offsets), 1)

    def piece(self, axes, offsets):
        index = 0
        for axis in axes:
            by = dict(offsets).get(axis, 0)
            index = index * LENGTH[axis] + lax.rem(self.at[axis] + by, LENGTH[axis])
        return index

    def chunk(self, tag, levels, base, size, start_time, prepare, square, finish):
        at = self.at
        starts, sizes, kinds = [base], [size], []
        for level in levels:
            kind, axes = level.split(":")
            kinds.append((kind, axes))
            sizes.append(sizes[-1] // math.prod(LENGTH[a] for a in axes))
            starts.append(starts[-1] + self.piece(axes, ()) * sizes[-1])
        waits, cost = [], 0.15
        for i, (kind, axes) in enumerate(kinds):
            args = (tag, i, axes, starts[i], sizes[i + 1], starts[i + 1])
            reduce = self.reduce_ring if kind == "r" else self.reduce_direct
            waits, prepare = reduce(args, waits, prepare, cost, start_time)
            start_time, cost = 0.0, 0.05

        def settle(add=prepare):
            add()
            square(starts[-1], sizes[-1])

        self.settled.append(("settled", tag))
        prepare, gives, stream = settle, ("settled", tag), []
        for i in reversed(range(len(kinds))):
            kind, axes = kinds[i]
            if i == 0 and axes == "x":
                waits, prepare = self.gather_stream(tag, waits, prepare, stream, sizes[1])
                continue
            args = (tag, i, axes, starts[i], sizes[i + 1], starts[i + 1])
            onward = i == 1 and kinds[0][1] == "x"
            build = self.gather_ring if kind == "r" else self.gather_direct
            waits, prepare, stream = build(args, waits, prepare, gives, onward)
            gives = None
        self.events.append(Event(waits, prepare, gives=("end", tag)))
        self.events.append(Event([("end", tag), "factor"], lambda: finish(base, size), cost=0.2))

    def reduce_direct(self, args, waits, prepare, cost, start_time):
        tag, i, axes, start, part, mine = args
        key, offsets = (tag, "rs", i), others(axes)
        places = [self.slot(part) for _ in offsets]
        for _ in offsets:
            self.expect(key, part, 0)

        def run():
            prepare()
            for o, place in zip(offsets, places):
                self.scatter(key, start + self.piece(axes, o) * part, place, part, o)

        sends = [self.copy_of(key, part, o) for o in offsets]
        self.events.append(Event(waits, run, sends, cost, start=start_time))

        def after():
            self.exchange.wait(key)
            self.add_into(mine, part, places)

        return [key], after

    def reduce_ring(self, args, waits, prepare, cost, start_time):
        tag, i, axis, start, part, mine = args
        half = part // 2
        far = {1: (tag, "far+"), 3: (tag, "far-")}
        near = (tag, "near")
        far_at = {1: self.slot(half), 3: self.slot(half)}
        near_at = {(by, h): self.slot(half) for by in (1, 3) for h in (0, 1)}
        for by in (1, 3):
            self.expect(far[by], half, 0)
            self.expect(near, part, 0)

        def quarter(by, h):
            return start + lax.rem(self.at[axis] + by, 4) * part + h * half

        def run():
            prepare()
            for by, h in ((1, 0), (3, 1)):
                self.scatter(far[by], quarter(2, h), far_at[by], half, ((axis, by),))
            for by, h in ((1, 1), (3, 0)):
                self.scatter(near, quarter(by, h), near_at[by, h], half, ((axis, by),))

        sends = [self.copy_of(far[by], half, ((axis, by),)) for by in (1, 3)]
        sends += [self.copy_of(near, half, ((axis, by),)) for by in (1, 3)]
        self.events.append(Event(waits, run, sends, cost, start=start_time))
        for by, h in ((1, 0), (3, 1)):

            def pass_on(by=by, h=h):
                self.exchange.wait(far[by])
                self.add_into(quarter(by, h), half, [far_at[by]])
                self.scatter(near, quarter(by, h), near_at[by, h], half, ((axis, by),))

            self.events.append(Event([far[by]], pass_on, [self.copy_of(near, half, ((axis, by),))], 0.03))

        def after():
            self.exchange.wait(near)
            for h in (0, 1):
                self.add_into(mine + h * half, half, [near_at[1, h], near_at[3, h]])

        return [near], after

    def gather_direct(self, args, waits, prepare, gives, onward):
        tag, i, axes, _, part, mine = args
        key, offsets = (tag, "ag", i), others(axes)
        for _ in offsets:
            self.expect(key, part, 1)

        def run():
            prepare()
            for o in offsets:
                self.gather(key, mine, part, o)

        self.events.append(Event(waits, run, [self.copy_of(key, part, o) for o in offsets], 0.05, gives))
        return [key], lambda: self.exchange.wait(key), None

    def gather_ring(self, args, waits, prepare, gives, onward):
        tag, i, axis, start, part, mine = args
        half = part // 2
        on = {1: (tag, "on+"), 3: (tag, "on-")}
        end, cross = (tag, "end"), (tag, "cross")
        across = (("x", 1),)
        for by in (1, 3):
            self.expect(on[by], half, 1)
            self.expect(end, part, 1)
        if onward:
            self.expect(cross, 4 * part, 1)

        def quarter(by, h):
            return start + lax.rem(self.at[axis] + by, 4) * part + h * half

        def run():
            prepare()
            for by, h in ((1, 0), (3, 1)):
                self.gather(on[by], mine + h * half, half, ((axis, by),))
            for by, h in ((1, 1), (3, 0)):
                self.gather(end, mine + h * half, half, ((axis, by),))
            if onward:
                self.gather(cross, mine, part, across)

        sends = [self.copy_of(on[by], half, ((axis, by),)) for by in (1, 3)]
        sends += [self.copy_of(end, half, ((axis, by),)) for by in (1, 3)]
        sends += [self.copy_of(cross, part, across)] * onward
        self.events.append(Event(waits, run, sends, 0.05, gives))
        for by, h in ((1, 0), (3, 1)):

            def pass_on(by=by, h=h):
                self.exchange.wait(on[by])
                self.gather(end, quarter(4 - by, h), half, ((axis, by),))
                if onward:
                    self.gather(cross, quarter(4 - by, h), half, across)

            sends = [self.copy_of(end, half, ((axis, by),))]
            sends += [self.copy_of(cross, half, across)] * onward
            self.events.append(Event([on[by]], pass_on, sends, 0.03))

        def after():
            self.exchange.wait(end)

        def stream():
            self.gather(cross, quarter(3, 1), half, across)
            self.gather(cross, quarter(1, 0), half, across)
            self.gather(cross, quarter(2, 0), part, across)

        return [end], after, (stream, [half, half, part])

    def gather_stream(self, tag, waits, prepare, stream, size):
        stream, parts = stream
        key = (tag, "cross")

        def run():
            prepare()
            stream()

        self.events.append(Event(waits, run, [self.copy_of(key, n, (("x", 1),)) for n in parts], 0.05))
        return [key], lambda: self.exchange.wait(key)


def norm_events(at, settled, squares, parts, recv_sems, send_sem, finish):
    events, base, friends = [], 0, []
    mp = lax.axis_index("mp")
    rounds = [[(moved(at, o), o) for o in others(axis)] for axis in "yz"]
    last = []
    for flip in (0, 1):
        for by in range(4):
            if flip or by:
                o = (("x", 1),)
                last.append((dict(moved(at, o if flip else ()), mp=lax.rem(mp + by, 4)), o))
    rounds.append(last)
    waits = settled
    for i, peers in enumerate(rounds):
        key, part = ("norm", i), pl.ds(base, len(peers))

        def run(i=i, peers=peers, base=base):
            if i:
                add(i - 1)
            for j, (device, _) in enumerate(peers):
                pltpu.make_async_remote_copy(
                    src_ref=squares.at[i],
                    dst_ref=parts.at[base + j],
                    send_sem=send_sem,
                    recv_sem=recv_sems.at[i],
                    device_id=device,
                    device_id_type=MESH,
                ).start()

        events.append(Event(waits, run, [(key, 4096, o) for _, o in peers], 0.05))
        waits, base = [key], base + len(peers)
        friends += [device for device, _ in peers]

    def add(i):
        start = sum(len(p) for p in rounds[:i])
        n = len(rounds[i])
        part = parts.at[pl.ds(start, n)]
        pltpu.make_async_copy(part, part, recv_sems.at[i]).wait()
        value = squares[i]
        for j in range(n):
            value = value + parts[start + j]
        squares[i + 1] = value

    def end():
        add(2)
        finish()

    events.append(Event(waits, end, cost=0.2, gives="factor"))

    def drain():
        pltpu.make_async_copy(parts, parts, send_sem).wait()

    return events, friends, drain


def kernel(
    max_norm, count, slow, fast, momentum, slow_out, momentum_out, fast_out,
    slow_in, fast_in, momentum_in, diff, recv, total, squares, parts, factor,
    load_sems, recv_sems, send_sems, norm_sems,
):
    dp = lax.axis_index("dp")
    at = {"y": dp // 8, "z": lax.rem(dp // 2, 4), "x": lax.rem(dp, 2)}
    loads, base = [], 0
    for i, size in enumerate(LOADS):
        part = pl.ds(base, size)
        pair = []
        for j, (src, dst) in enumerate(((slow, slow_in), (fast, fast_in))):
            pair.append(pltpu.make_async_copy(src.at[part], dst.at[part], load_sems.at[2 * i + j]))
            pair[-1].start()
        loads.append((base + size, pair))
        base += size
    late = pltpu.make_async_copy(momentum, momentum_in, load_sems.at[2 * len(LOADS)])
    late.start()
    squares[0] = jnp.zeros(squares.shape[1:], squares.dtype)

    def load(base, size):
        def run():
            while loads and (not ready[0] or ready[0] < base + size):
                ready[0], pair = loads.pop(0)
                for copy in pair:
                    copy.wait()
            part = pl.ds(base, size)
            diff[part] = slow_in[part] - fast_in[part].astype(jnp.float32)

        return run

    ready = [0]

    def square(start, size):
        value = diff[rows(start, size)]
        total[rows(start, size)] = value
        value = value * value
        value = value[:, :128] + value[:, 128:]
        squares[0] += value.reshape(size // 8, 8, 128).sum(axis=0)

    def clip():
        norm = jnp.sqrt(jnp.sum(squares[3], axis=(0, 1), keepdims=True)) / count
        scale = jnp.minimum(1.0, max_norm / (norm + EPSILON)) / count
        factor[...] = jnp.broadcast_to(scale, factor.shape)
        late.wait()

    def finish(base, size):
        part = pl.ds(base, size)
        scale = jnp.concatenate([factor[0:1], factor[0:1]], axis=1)
        gradient = scale * total[part]
        momentum_next = MOMENTUM_RATE * momentum_in[part] + gradient
        slow_next = slow_in[part] - OUTER_RATE * (gradient + MOMENTUM_RATE * momentum_next)
        momentum_out[part] = momentum_next
        slow_out[part] = slow_next
        fast_out[part] = slow_next.astype(fast_out.dtype)

    exchange = Exchange(recv_sems, send_sems, total)
    work = Sum(at, exchange, diff, recv, total)
    base = 0
    for tag, (levels, size, start_time) in enumerate(CHUNKS):
        work.chunk(tag, levels, base, size, start_time, load(base, size), square, finish)
        base += size
    events, friends, drain = norm_events(
        at, work.settled, squares, parts, norm_sems, send_sems.at[2], clip
    )
    events, _ = in_order(work.events + events)

    met = {o for o in others("zx") + others("yx")}
    friends = [moved(at, o) for o in sorted(met) if o != (("x", 1),)] + friends[6:]
    barrier = pltpu.get_barrier_semaphore()
    for device in friends:
        pl.semaphore_signal(barrier, inc=1, device_id=device, device_id_type=MESH)
    pl.semaphore_wait(barrier, len(friends))

    for event in events:
        event.run()
    exchange.drain(0)
    exchange.drain(1)
    drain()


def updated(slow, fast, momentum, max_norm, count):
    f32, shape = jnp.float32, slow.shape
    hbm = pl.BlockSpec(memory_space=pltpu.HBM)
    vmem = pl.BlockSpec(memory_space=pltpu.VMEM)
    groups = sum(8 if len(levels) == 2 else 10 for levels, _, _ in CHUNKS)
    return pl.pallas_call(
        lambda *refs: kernel(max_norm, count, *refs),
        out_shape=(pltpu.VMEM(shape, f32), pltpu.VMEM(shape, f32), pltpu.VMEM(shape, fast.dtype)),
        in_specs=[hbm, hbm, hbm],
        out_specs=(vmem, vmem, vmem),
        scratch_shapes=[
            pltpu.VMEM(shape, f32),
            pltpu.VMEM(shape, fast.dtype),
            pltpu.VMEM(shape, f32),
            pltpu.VMEM(shape, f32),
            pltpu.VMEM(shape, f32),
            pltpu.VMEM(shape, f32),
            pltpu.VMEM((4, 8, 128), f32),
            pltpu.VMEM((13, 8, 128), f32),
            pltpu.VMEM((8, 128), f32),
            pltpu.SemaphoreType.DMA((2 * len(LOADS) + 1,)),
            pltpu.SemaphoreType.DMA((groups,)),
            pltpu.SemaphoreType.DMA((3,)),
            pltpu.SemaphoreType.DMA((3,)),
        ],
        compiler_params=pltpu.CompilerParams(
            collective_id=0, has_side_effects=True, vmem_limit_bytes=40 * 1024 * 1024
        ),
        name="updated",
    )(*(pltpu.with_memory_space_constraint(x, pltpu.HBM) for x in (slow, fast, momentum)))


def body(slow_weights, fast_weights, momentum):
    replicas = lax.axis_size("dp")
    entries = slow_weights.shape[0] * slow_weights.shape[1] * slow_weights.shape[2] * lax.axis_size("mp")
    max_norm = CLIP_LEVEL * math.sqrt(entries)
    slow_next, momentum_next, fast_next = updated(
        slow_weights[0], fast_weights[0, 0], momentum[0], max_norm, replicas
    )
    return (slow_next[None], momentum_next[None], fast_next[None, None])


def solution(mesh):
    in_specs = (P(None, None, "mp"), P("dp", None, None, "mp"), P(None, None, "mp"))
    out_specs = (P(None, None, "mp"), P(None, None, "mp"), P("dp", None, None, "mp"))
    return jax.shard_map(body, mesh=mesh, in_specs=in_specs, out_specs=out_specs, check_vma=False)
```

time: 135 us -> 58.1 us (0.43)
  blocking collectives: 114 us -> 0 us
  Pallas kernels: 0 us -> 52.4 us
  other arithmetic: 14.4 us -> 0 us
    all_to_all x3 -> x0, blocking collectives: 114 us -> none  [the longest x1 58.3 us: sent_and_summed(): lax.all_to_all(parts, axis, split_axis=0, concat_axis=0, tiled=True)]
    pallas_call x0 -> x1, Pallas kernels: none -> 52.4 us  [updated(): pl.pallas_call(lambda *refs: kernel(max_norm, count, *refs), out_shape=(p...]
    broadcast_in_dim x1 -> x0, other arithmetic: 4.58 us -> none  [body(): fast_next = slow_next.astype(jnp.bfloat16)[None]]
    reduce_sum x3 -> x0, other arithmetic: 4.41 us -> none  [the longest x1 2.26 us: sent_and_summed(): return arrived.sum(axis=0)]
    sub x1 -> x0, other arithmetic: 2.97 us -> none  [body(): difference = slow_weights - fast_weights[0].astype(jnp.float32)]
    mul x1 -> x0, other arithmetic: 2.44 us -> none  [apply_update(): gradient = factor * pseudo]
    unnamed x6 -> x3, local copies, waits for them, and re-layouts: 3.64 us -> 4.9 us
where the time goes in v2:
time: 58.1 us; the launch traced here: 57.9 us
  Pallas kernels  52.4 us (90%)
  local copies, waits for them, and re-layouts  4.9 us (8%)
  between operations  0.64 us (1%)
    pallas_call x1, Pallas kernels, updated(): pl.pallas_call(lambda *refs: kernel(max_norm, count, *refs), out_shape=(p...  52.4 us
    unnamed x3, local copies, waits for them, and re-layouts  4.9 us

profile of v2, /device:TPU:0, one launch (start us, length us, event | category | flops | bytes accessed | tf_op | source)
XLA Modules:
  0.0 57.9 jit_solution(11153574606858651172)
XLA Ops:
  0.6 52.4 %updated.1 = (f32[3584,256]{1,0:T(8,128)S(1)}, f32[3584,256]{1,0:T(8,128)S(1)}, bf16[3584,256]{1,0:T(8,128)(2,1)S(1)}) custom-call(f32[3584,256]{1,0:T(8,128)} %bitcast.9, bf16[3584,256]{1,0:T(8,128)(2,1)} %bitcast.11, f32[3584,256]{1,0:T(8,128)} %bitcast.10), custom_call_target="tpu_custom_call" | custom-call | tf_op jit(solution)/shard_map/updated/pallas_call | solution.py:469
  53.0 1.8 %copy.9 = f32[1,3584,256]{2,1,0:T(8,128)} copy(f32[1,3584,256]{2,1,0:T(8,128)S(1)} %bitcast.7) | data formatting | bytes 7340032
  54.9 1.8 %copy.10 = f32[1,3584,256]{2,1,0:T(8,128)} copy(f32[1,3584,256]{2,1,0:T(8,128)S(1)} %bitcast.6) | data formatting | bytes 7340032
  56.7 1.2 %copy.11 = bf16[1,1,3584,256]{3,2,1,0:T(8,128)(2,1)} copy(bf16[1,1,3584,256]{3,2,1,0:T(8,128)(2,1)S(1)} %bitcast.8) | data formatting | bytes 3670016

commit v3 on v2

--- a/solution.py
+++ b/solution.py
@@ -17,17 +17,11 @@
 COLUMNS = 256
 Y, Z = ("r:y", "d:zx"), ("r:z", "d:yx")
 XY, XZ = ("d:x", "r:y", "d:z"), ("d:x", "r:z", "d:y")
-CHUNKS = (
-    (XY, 256, 0.0), (Y, 256, 0.0), (Z, 256, 0.0), (XZ, 256, 0.0),
-    (Y, 256, 0.0), (Z, 256, 0.0), (XY, 256, 0.0),
-    (Y, 256, 0.0), (Z, 256, 0.0), (XZ, 256, 0.0),
-    (Y, 256, 0.0), (Z, 256, 0.0),
-    (Y, 256, 0.0), (Z, 256, 0.0),
-)
+CHUNKS = ((('d:x', 'd:y', 'd:z'), 256, False, ((-1, 21.5),)), (('r:y', 'd:zx'), 256, True, ((-2, 18.3), (-1, 21.4), (0, 1.8), (1, 2.9))), (('d:x', 'd:z', 'd:y'), 256, True, ((-1, 16.4), (0, 1.0), (1, 3.0))), (('r:y', 'd:zx'), 256, True, ((-3, 16.1), (-1, 5.4), (0, 9.9))), (('r:z', 'd:yx'), 256, False, ((-2, 6.7),)), (('r:y', 'd:z', 'd:x'), 256, True, ((-3, 15.6), (-2, 14.7), (-1, 7.1), (1, 9.9))), (('r:z', 'd:yx'), 256, False, ((-3, 5.8), (-2, 21.7), (-1, 0.4), (0, 0), (1, 16.5))), (('d:x', 'r:y', 'd:z'), 256, False, ((-1, 31.0),)), (('r:y', 'd:zx'), 256, True, ((-3, 8.3), (-1, 13.4), (0, 8.0))), (('r:z', 'd:y', 'd:x'), 512, True, ((-1, 23.5),)), (('r:z', 'd:y', 'd:x'), 256, False, ()), (('r:y', 'd:z', 'd:x'), 256, True, ((-3, 3.0), (-2, 4.1), (-1, 17.6), (1, 13.8))), (('d:x', 'd:z', 'd:y'), 256, False, ((-3, 5.2), (0, 6.9), (1, 2.3))))
 LOADS = (768, 1024, 896, 896)
 RATE = 46.6e3
-HOP = (1.6, 0.6)
-ISSUE = 0.03
+HOP = (2.1, 0.6)
+ISSUE = 0.02
 
 
 class Event:
@@ -155,20 +149,20 @@
             index = index * LENGTH[axis] + lax.rem(self.at[axis] + by, LENGTH[axis])
         return index
 
-    def chunk(self, tag, levels, base, size, start_time, prepare, square, finish):
-        at = self.at
+    def chunk(self, tag, levels, base, size, early, times, prepare, square, finish):
+        self.early = early
         starts, sizes, kinds = [base], [size], []
         for level in levels:
             kind, axes = level.split(":")
             kinds.append((kind, axes))
             sizes.append(sizes[-1] // math.prod(LENGTH[a] for a in axes))
             starts.append(starts[-1] + self.piece(axes, ()) * sizes[-1])
-        waits, cost = [], 0.15
+        waits, cost, times = [], 0.15, dict(times)
         for i, (kind, axes) in enumerate(kinds):
             args = (tag, i, axes, starts[i], sizes[i + 1], starts[i + 1])
             reduce = self.reduce_ring if kind == "r" else self.reduce_direct
-            waits, prepare = reduce(args, waits, prepare, cost, start_time)
-            start_time, cost = 0.0, 0.05
+            waits, prepare = reduce(args, waits, prepare, cost, times.get(i, 0.0))
+            cost = 0.05
 
         def settle(add=prepare):
             add()
@@ -178,13 +172,15 @@
         prepare, gives, stream = settle, ("settled", tag), []
         for i in reversed(range(len(kinds))):
             kind, axes = kinds[i]
-            if i == 0 and axes == "x":
+            if i == 0 and stream:
                 waits, prepare = self.gather_stream(tag, waits, prepare, stream, sizes[1])
                 continue
             args = (tag, i, axes, starts[i], sizes[i + 1], starts[i + 1])
-            onward = i == 1 and kinds[0][1] == "x"
+            onward = i == 1 and kinds[0][1] == "x" and kind == "r"
             build = self.gather_ring if kind == "r" else self.gather_direct
+            begun = len(self.events)
             waits, prepare, stream = build(args, waits, prepare, gives, onward)
+            self.events[begun].start = times.get(-1 - i, 0.0)
             gives = None
         self.events.append(Event(waits, prepare, gives=("end", tag)))
         self.events.append(Event([("end", tag), "factor"], lambda: finish(base, size), cost=0.2))
@@ -212,9 +208,9 @@
 
     def reduce_ring(self, args, waits, prepare, cost, start_time):
         tag, i, axis, start, part, mine = args
-        half = part // 2
-        far = {1: (tag, "far+"), 3: (tag, "far-")}
-        near = (tag, "near")
+        half, early = part // 2, self.early
+        far = {1: (tag, "far+", i), 3: (tag, "far-", i)}
+        near = (tag, "near", i)
         far_at = {1: self.slot(half), 3: self.slot(half)}
         near_at = {(by, h): self.slot(half) for by in (1, 3) for h in (0, 1)}
         for by in (1, 3):
@@ -228,20 +224,23 @@
             prepare()
             for by, h in ((1, 0), (3, 1)):
                 self.scatter(far[by], quarter(2, h), far_at[by], half, ((axis, by),))
-            for by, h in ((1, 1), (3, 0)):
-                self.scatter(near, quarter(by, h), near_at[by, h], half, ((axis, by),))
+            if early:
+                for by, h in ((1, 1), (3, 0)):
+                    self.scatter(near, quarter(by, h), near_at[by, h], half, ((axis, by),))
 
         sends = [self.copy_of(far[by], half, ((axis, by),)) for by in (1, 3)]
-        sends += [self.copy_of(near, half, ((axis, by),)) for by in (1, 3)]
+        sends += [self.copy_of(near, half, ((axis, by),)) for by in (1, 3)] * early
         self.events.append(Event(waits, run, sends, cost, start=start_time))
         for by, h in ((1, 0), (3, 1)):
 
             def pass_on(by=by, h=h):
                 self.exchange.wait(far[by])
                 self.add_into(quarter(by, h), half, [far_at[by]])
-                self.scatter(near, quarter(by, h), near_at[by, h], half, ((axis, by),))
-
-            self.events.append(Event([far[by]], pass_on, [self.copy_of(near, half, ((axis, by),))], 0.03))
+                for k in (h,) if early else (h, 1 - h):
+                    self.scatter(near, quarter(by, k), near_at[by, k], half, ((axis, by),))
+
+            sends = [self.copy_of(near, half, ((axis, by),))] * (1 if early else 2)
+            self.events.append(Event([far[by]], pass_on, sends, 0.03))
 
         def after():
             self.exchange.wait(near)
@@ -267,8 +266,8 @@
     def gather_ring(self, args, waits, prepare, gives, onward):
         tag, i, axis, start, part, mine = args
         half = part // 2
-        on = {1: (tag, "on+"), 3: (tag, "on-")}
-        end, cross = (tag, "end"), (tag, "cross")
+        on = {1: (tag, "on+", i), 3: (tag, "on-", i)}
+        end, cross = (tag, "end", i), (tag, "cross")
         across = (("x", 1),)
         for by in (1, 3):
             self.expect(on[by], half, 1)
@@ -312,7 +311,7 @@
             self.gather(cross, quarter(1, 0), half, across)
             self.gather(cross, quarter(2, 0), part, across)
 
-        return [end], after, (stream, [half, half, part])
+        return [end], after, (stream, [half, half, part]) if onward else None
 
     def gather_stream(self, tag, waits, prepare, stream, size):
         stream, parts = stream
@@ -329,7 +328,7 @@
 def norm_events(at, settled, squares, parts, recv_sems, send_sem, finish):
     events, base, friends = [], 0, []
     mp = lax.axis_index("mp")
-    rounds = [[(moved(at, o), o) for o in others(axis)] for axis in "yz"]
+    rounds = [[(moved(at, o), o) for o in others("yz")]]
     last = []
     for flip in (0, 1):
         for by in range(4):
@@ -369,7 +368,7 @@
         squares[i + 1] = value
 
     def end():
-        add(2)
+        add(1)
         finish()
 
     events.append(Event(waits, end, cost=0.2, gives="factor"))
@@ -421,7 +420,7 @@
         squares[0] += value.reshape(size // 8, 8, 128).sum(axis=0)
 
     def clip():
-        norm = jnp.sqrt(jnp.sum(squares[3], axis=(0, 1), keepdims=True)) / count
+        norm = jnp.sqrt(jnp.sum(squares[2], axis=(0, 1), keepdims=True)) / count
         scale = jnp.minimum(1.0, max_norm / (norm + EPSILON)) / count
         factor[...] = jnp.broadcast_to(scale, factor.shape)
         late.wait()
@@ -439,16 +438,15 @@
     exchange = Exchange(recv_sems, send_sems, total)
     work = Sum(at, exchange, diff, recv, total)
     base = 0
-    for tag, (levels, size, start_time) in enumerate(CHUNKS):
-        work.chunk(tag, levels, base, size, start_time, load(base, size), square, finish)
+    for tag, (levels, size, early, times) in enumerate(CHUNKS):
+        work.chunk(tag, levels, base, size, early, times, load(base, size), square, finish)
         base += size
     events, friends, drain = norm_events(
         at, work.settled, squares, parts, norm_sems, send_sems.at[2], clip
     )
     events, _ = in_order(work.events + events)
 
-    met = {o for o in others("zx") + others("yx")}
-    friends = [moved(at, o) for o in sorted(met) if o != (("x", 1),)] + friends[6:]
+    friends += [moved(at, o) for o in others("yzx") if o[-1][0] == "x" and len(o) > 1]
     barrier = pltpu.get_barrier_semaphore()
     for device in friends:
         pl.semaphore_signal(barrier, inc=1, device_id=device, device_id_type=MESH)
@@ -465,7 +463,7 @@
     f32, shape = jnp.float32, slow.shape
     hbm = pl.BlockSpec(memory_space=pltpu.HBM)
     vmem = pl.BlockSpec(memory_space=pltpu.VMEM)
-    groups = sum(8 if len(levels) == 2 else 10 for levels, _, _ in CHUNKS)
+    groups = sum(2 if level[0] == "d" else 6 for chunk in CHUNKS for level in chunk[0])
     return pl.pallas_call(
         lambda *refs: kernel(max_norm, count, *refs),
         out_shape=(pltpu.VMEM(shape, f32), pltpu.VMEM(shape, f32), pltpu.VMEM(shape, fast.dtype)),
@@ -478,13 +476,13 @@
             pltpu.VMEM(shape, f32),
             pltpu.VMEM(shape, f32),
             pltpu.VMEM(shape, f32),
-            pltpu.VMEM((4, 8, 128), f32),
-            pltpu.VMEM((13, 8, 128), f32),
+            pltpu.VMEM((3, 8, 128), f32),
+            pltpu.VMEM((22, 8, 128), f32),
             pltpu.VMEM((8, 128), f32),
             pltpu.SemaphoreType.DMA((2 * len(LOADS) + 1,)),
             pltpu.SemaphoreType.DMA((groups,)),
             pltpu.SemaphoreType.DMA((3,)),
-            pltpu.SemaphoreType.DMA((3,)),
+            pltpu.SemaphoreType.DMA((2,)),
         ],
         compiler_params=pltpu.CompilerParams(
             collective_id=0, has_side_effects=True, vmem_limit_bytes=40 * 1024 * 1024
@@ -493,13 +491,32 @@
     )(*(pltpu.with_memory_space_constraint(x, pltpu.HBM) for x in (slow, fast, momentum)))
 
 
+def written(*values):
+    def run(*refs):
+        n = len(values)
+        copies = [pltpu.make_async_copy(refs[i], refs[n + i], refs[-1].at[i]) for i in range(n)]
+        for copy in copies:
+            copy.start()
+        for copy in copies:
+            copy.wait()
+
+    return pl.pallas_call(
+        run,
+        out_shape=tuple(pltpu.HBM(x.shape, x.dtype) for x in values),
+        in_specs=[pl.BlockSpec(memory_space=pltpu.VMEM)] * len(values),
+        out_specs=tuple(pl.BlockSpec(memory_space=pltpu.HBM) for _ in values),
+        scratch_shapes=[pltpu.SemaphoreType.DMA((len(values),))],
+        compiler_params=pltpu.CompilerParams(vmem_limit_bytes=1024 * 1024),
+        name="written",
+    )(*(pltpu.with_memory_space_constraint(x, pltpu.VMEM) for x in values))
+
+
 def body(slow_weights, fast_weights, momentum):
     replicas = lax.axis_size("dp")
     entries = slow_weights.shape[0] * slow_weights.shape[1] * slow_weights.shape[2] * lax.axis_size("mp")
     max_norm = CLIP_LEVEL * math.sqrt(entries)
-    slow_next, momentum_next, fast_next = updated(
-        slow_weights[0], fast_weights[0, 0], momentum[0], max_norm, replicas
-    )
+    values = updated(slow_weights[0], fast_weights[0, 0], momentum[0], max_norm, replicas)
+    slow_next, momentum_next, fast_next = written(*values)
     return (slow_next[None], momentum_next[None], fast_next[None, None])
 
 

time: 58.1 us -> 54.8 us (0.943)
  local copies, waits for them, and re-layouts: 4.9 us -> 0 us
  Pallas kernels: 52.4 us -> 54 us
    unnamed x3 -> x0, local copies, waits for them, and re-layouts: 4.9 us -> none
    pallas_call x0 -> x1, Pallas kernels: none -> 3.67 us  [written(): pl.pallas_call(run, out_shape=tuple((pltpu.HBM(x.shape, x.dtype) for x in...]
    pallas_call x1, Pallas kernels: 52.4 us -> 50.3 us  [updated(): pl.pallas_call(lambda *refs: kernel(max_norm, count, *refs), out_shape=(p...]
where the time goes in v3:
time: 54.8 us; the launch traced here: 54.7 us
  Pallas kernels  54 us (99%)
  between operations  0.64 us (1%)
    pallas_call x1, Pallas kernels, updated(): pl.pallas_call(lambda *refs: kernel(max_norm, count, *refs), out_shape=(p...  50.3 us
    pallas_call x1, Pallas kernels, written(): pl.pallas_call(run, out_shape=tuple((pltpu.HBM(x.shape, x.dtype) for x in...  3.67 us

profile of v3, /device:TPU:0, one launch (start us, length us, event | category | flops | bytes accessed | tf_op | source)
XLA Modules:
  0.0 54.7 jit_solution(18083433172108673832)
XLA Ops:
  0.6 50.3 %updated.1 = (f32[3584,256]{1,0:T(8,128)S(1)}, f32[3584,256]{1,0:T(8,128)S(1)}, bf16[3584,256]{1,0:T(8,128)(2,1)S(1)}) custom-call(f32[3584,256]{1,0:T(8,128)} %bitcast.6, bf16[3584,256]{1,0:T(8,128)(2,1)} %bitcast.8, f32[3584,256]{1,0:T(8,128)} %bitcast.7), custom_call_target="tpu_custom_call" | custom-call | tf_op jit(solution)/shard_map/updated/pallas_call | solution.py:467
  51.0 3.7 %written.1 = (f32[3584,256]{1,0:T(8,128)}, f32[3584,256]{1,0:T(8,128)}, bf16[3584,256]{1,0:T(8,128)(2,1)}) custom-call(f32[3584,256]{1,0:T(8,128)S(1)} %get-tuple-element.9.refs_0_, f32[3584,256]{1,0:T(8,128)S(1)} %get-tuple-element.10.refs_1_, bf16[3584,256]{1,0:T(8,128)(2,1)S(1)} %get-tuple-element.11.refs_2_), custom_call_target="tpu_custom_call" | custom-call | tf_op jit(solution)/shard_map/written/pallas_call | solution.py:503

commit v4 on v3

--- a/solution.py
+++ b/solution.py
@@ -17,11 +17,12 @@
 COLUMNS = 256
 Y, Z = ("r:y", "d:zx"), ("r:z", "d:yx")
 XY, XZ = ("d:x", "r:y", "d:z"), ("d:x", "r:z", "d:y")
-CHUNKS = ((('d:x', 'd:y', 'd:z'), 256, False, ((-1, 21.5),)), (('r:y', 'd:zx'), 256, True, ((-2, 18.3), (-1, 21.4), (0, 1.8), (1, 2.9))), (('d:x', 'd:z', 'd:y'), 256, True, ((-1, 16.4), (0, 1.0), (1, 3.0))), (('r:y', 'd:zx'), 256, True, ((-3, 16.1), (-1, 5.4), (0, 9.9))), (('r:z', 'd:yx'), 256, False, ((-2, 6.7),)), (('r:y', 'd:z', 'd:x'), 256, True, ((-3, 15.6), (-2, 14.7), (-1, 7.1), (1, 9.9))), (('r:z', 'd:yx'), 256, False, ((-3, 5.8), (-2, 21.7), (-1, 0.4), (0, 0), (1, 16.5))), (('d:x', 'r:y', 'd:z'), 256, False, ((-1, 31.0),)), (('r:y', 'd:zx'), 256, True, ((-3, 8.3), (-1, 13.4), (0, 8.0))), (('r:z', 'd:y', 'd:x'), 512, True, ((-1, 23.5),)), (('r:z', 'd:y', 'd:x'), 256, False, ()), (('r:y', 'd:z', 'd:x'), 256, True, ((-3, 3.0), (-2, 4.1), (-1, 17.6), (1, 13.8))), (('d:x', 'd:z', 'd:y'), 256, False, ((-3, 5.2), (0, 6.9), (1, 2.3))))
-LOADS = (768, 1024, 896, 896)
-RATE = 46.6e3
-HOP = (2.1, 0.6)
-ISSUE = 0.02
+CHUNKS = ((('r:z', 'd:x', 'd:y'), 256, False, ((-3, 3.8), (-2, 21.5), (-1, 5.5))), (('r:y', 'd:zx'), 256, True, ((-3, 0), (-1, 24.3), (0, 2.4))), (('r:y', 'd:x', 'd:z'), 256, False, ((-3, 7.3), (-2, 20.8), (-1, 24.4), (1, 2.7))), (('r:z', 'd:x', 'd:y'), 256, False, ((-3, 17.4), (-2, 11.1), (-1, 16.4), (1, 1.7))), (('r:y', 'd:zx'), 256, True, ((-3, 25.2), (-2, 3.6), (-1, 14.7), (1, 9.6))), (('d:x', 'r:z', 'd:y'), 256, False, ((-3, 1.7), (-1, 14.7), (1, 1.0))), (('r:y', 'd:zx'), 256, False, ((-3, 21.7), (-2, 18.7), (-1, 15.2), (1, 10.1))), (('r:z', 'd:x', 'd:y'), 256, True, ((-3, 20.1), (-2, 0), (-1, 5.5))), (('r:z', 'd:yx'), 256, True, ((-2, 12.5), (-1, 13.4), (0, 1.3), (1, 14.0))), (('d:x', 'd:y', 'd:z'), 256, True, ((-3, 5.6), (-1, 13.5), (0, 3.2), (1, 0.2))), (('r:y', 'd:zx'), 256, True, ((-2, 10.2), (-1, 4.9), (0, 5.1), (1, 11.6))), (('r:y', 'd:zx'), 256, True, ((-2, 0), (-1, 12.0))), (('r:z', 'd:x', 'd:y'), 256, True, ((-1, 20.7),)), (('d:x', 'd:z', 'd:y'), 256, False, ((-3, 5.2),)))
+LOADS = (512, 768, 1024, 1280)
+RATE = 45e3
+HOP = (2.7, 0.5)
+ISSUE = 0.01
+COST = 0.4
 
 
 class Event:
@@ -46,7 +47,7 @@
         ready, event = best
         left.remove(event)
         done.append(event)
-        now = max(now, ready) + event.cost
+        now = max(now, ready) + COST * event.cost
         for key, size, hops in event.sends:
             now += ISSUE
             end = now
@@ -209,12 +210,12 @@
     def reduce_ring(self, args, waits, prepare, cost, start_time):
         tag, i, axis, start, part, mine = args
         half, early = part // 2, self.early
-        far = {1: (tag, "far+", i), 3: (tag, "far-", i)}
+        far = (tag, "far", i)
         near = (tag, "near", i)
         far_at = {1: self.slot(half), 3: self.slot(half)}
         near_at = {(by, h): self.slot(half) for by in (1, 3) for h in (0, 1)}
         for by in (1, 3):
-            self.expect(far[by], half, 0)
+            self.expect(far, half, 0)
             self.expect(near, part, 0)
 
         def quarter(by, h):
@@ -223,24 +224,24 @@
         def run():
             prepare()
             for by, h in ((1, 0), (3, 1)):
-                self.scatter(far[by], quarter(2, h), far_at[by], half, ((axis, by),))
+                self.scatter(far, quarter(2, h), far_at[by], half, ((axis, by),))
             if early:
                 for by, h in ((1, 1), (3, 0)):
                     self.scatter(near, quarter(by, h), near_at[by, h], half, ((axis, by),))
 
-        sends = [self.copy_of(far[by], half, ((axis, by),)) for by in (1, 3)]
+        sends = [self.copy_of(far, half, ((axis, by),)) for by in (1, 3)]
         sends += [self.copy_of(near, half, ((axis, by),)) for by in (1, 3)] * early
         self.events.append(Event(waits, run, sends, cost, start=start_time))
-        for by, h in ((1, 0), (3, 1)):
-
-            def pass_on(by=by, h=h):
-                self.exchange.wait(far[by])
+
+        def pass_on():
+            self.exchange.wait(far)
+            for by, h in ((1, 0), (3, 1)):
                 self.add_into(quarter(by, h), half, [far_at[by]])
-                for k in (h,) if early else (h, 1 - h):
-                    self.scatter(near, quarter(by, k), near_at[by, k], half, ((axis, by),))
-
-            sends = [self.copy_of(near, half, ((axis, by),))] * (1 if early else 2)
-            self.events.append(Event([far[by]], pass_on, sends, 0.03))
+            for by, h in ((1, 0), (3, 1)) if early else ((1, 0), (3, 1), (1, 1), (3, 0)):
+                self.scatter(near, quarter(by, h), near_at[by, h], half, ((axis, by),))
+
+        sends = [self.copy_of(near, half, ((axis, by),)) for by in (1, 3)]
+        self.events.append(Event([far], pass_on, sends * (1 if early else 2), 0.06))
 
         def after():
             self.exchange.wait(near)
@@ -266,11 +267,11 @@
     def gather_ring(self, args, waits, prepare, gives, onward):
         tag, i, axis, start, part, mine = args
         half = part // 2
-        on = {1: (tag, "on+", i), 3: (tag, "on-", i)}
+        on = (tag, "on", i)
         end, cross = (tag, "end", i), (tag, "cross")
         across = (("x", 1),)
         for by in (1, 3):
-            self.expect(on[by], half, 1)
+            self.expect(on, half, 1)
             self.expect(end, part, 1)
         if onward:
             self.expect(cross, 4 * part, 1)
@@ -281,27 +282,28 @@
         def run():
             prepare()
             for by, h in ((1, 0), (3, 1)):
-                self.gather(on[by], mine + h * half, half, ((axis, by),))
+                self.gather(on, mine + h * half, half, ((axis, by),))
             for by, h in ((1, 1), (3, 0)):
                 self.gather(end, mine + h * half, half, ((axis, by),))
             if onward:
                 self.gather(cross, mine, part, across)
 
-        sends = [self.copy_of(on[by], half, ((axis, by),)) for by in (1, 3)]
+        sends = [self.copy_of(on, half, ((axis, by),)) for by in (1, 3)]
         sends += [self.copy_of(end, half, ((axis, by),)) for by in (1, 3)]
         sends += [self.copy_of(cross, part, across)] * onward
         self.events.append(Event(waits, run, sends, 0.05, gives))
-        for by, h in ((1, 0), (3, 1)):
-
-            def pass_on(by=by, h=h):
-                self.exchange.wait(on[by])
+
+        def pass_on():
+            self.exchange.wait(on)
+            for by, h in ((1, 0), (3, 1)):
                 self.gather(end, quarter(4 - by, h), half, ((axis, by),))
-                if onward:
+            if onward:
+                for by, h in ((1, 0), (3, 1)):
                     self.gather(cross, quarter(4 - by, h), half, across)
 
-            sends = [self.copy_of(end, half, ((axis, by),))]
-            sends += [self.copy_of(cross, half, across)] * onward
-            self.events.append(Event([on[by]], pass_on, sends, 0.03))
+        sends = [self.copy_of(end, half, ((axis, by),)) for by in (1, 3)]
+        sends += [self.copy_of(cross, half, across)] * (2 * onward)
+        self.events.append(Event([on], pass_on, sends, 0.03))
 
         def after():
             self.exchange.wait(end)
@@ -396,7 +398,6 @@
         loads.append((base + size, pair))
         base += size
     late = pltpu.make_async_copy(momentum, momentum_in, load_sems.at[2 * len(LOADS)])
-    late.start()
     squares[0] = jnp.zeros(squares.shape[1:], squares.dtype)
 
     def load(base, size):
@@ -452,7 +453,9 @@
         pl.semaphore_signal(barrier, inc=1, device_id=device, device_id_type=MESH)
     pl.semaphore_wait(barrier, len(friends))
 
-    for event in events:
+    for i, event in enumerate(events):
+        if i == len(CHUNKS):
+            late.start()
         event.run()
     exchange.drain(0)
     exchange.drain(1)
@@ -463,7 +466,7 @@
     f32, shape = jnp.float32, slow.shape
     hbm = pl.BlockSpec(memory_space=pltpu.HBM)
     vmem = pl.BlockSpec(memory_space=pltpu.VMEM)
-    groups = sum(2 if level[0] == "d" else 6 for chunk in CHUNKS for level in chunk[0])
+    groups = sum(2 if level[0] == "d" else 4 for chunk in CHUNKS for level in chunk[0])
     return pl.pallas_call(
         lambda *refs: kernel(max_norm, count, *refs),
         out_shape=(pltpu.VMEM(shape, f32), pltpu.VMEM(shape, f32), pltpu.VMEM(shape, fast.dtype)),

time: 54.8 us -> 53.9 us (0.984)
  Pallas kernels: 54 us -> 53.1 us
    pallas_call x1, Pallas kernels: 50.3 us -> 49.4 us  [updated(): pl.pallas_call(lambda *refs: kernel(max_norm, count, *refs), out_shape=(p...]
where the time goes in v4:
time: 53.9 us; the launch traced here: 53.8 us
  Pallas kernels  53.1 us (99%)
  between operations  0.64 us (1%)
    pallas_call x1, Pallas kernels, updated(): pl.pallas_call(lambda *refs: kernel(max_norm, count, *refs), out_shape=(p...  49.4 us
    pallas_call x1, Pallas kernels, written(): pl.pallas_call(run, out_shape=tuple((pltpu.HBM(x.shape, x.dtype) for x in...  3.67 us

profile of v4, /device:TPU:0, one launch (start us, length us, event | category | flops | bytes accessed | tf_op | source)
XLA Modules:
  0.0 53.8 jit_solution(10761759555875423165)
XLA Ops:
  0.6 49.4 %updated.1 = (f32[3584,256]{1,0:T(8,128)S(1)}, f32[3584,256]{1,0:T(8,128)S(1)}, bf16[3584,256]{1,0:T(8,128)(2,1)S(1)}) custom-call(f32[3584,256]{1,0:T(8,128)} %bitcast.6, bf16[3584,256]{1,0:T(8,128)(2,1)} %bitcast.8, f32[3584,256]{1,0:T(8,128)} %bitcast.7), custom_call_target="tpu_custom_call" | custom-call | tf_op jit(solution)/shard_map/updated/pallas_call | solution.py:470
  50.1 3.7 %written.1 = (f32[3584,256]{1,0:T(8,128)}, f32[3584,256]{1,0:T(8,128)}, bf16[3584,256]{1,0:T(8,128)(2,1)}) custom-call(f32[3584,256]{1,0:T(8,128)S(1)} %get-tuple-element.9.refs_0_, f32[3584,256]{1,0:T(8,128)S(1)} %get-tuple-element.10.refs_1_, bf16[3584,256]{1,0:T(8,128)(2,1)S(1)} %get-tuple-element.11.refs_2_), custom_call_target="tpu_custom_call" | custom-call | tf_op jit(solution)/shard_map/written/pallas_call | solution.py:506

commit v5 on v4

--- a/solution.py
+++ b/solution.py
@@ -79,6 +79,10 @@
     return [tuple((a, by) for a, by in o if by) for o in found if any(by for _, by in o)]
 
 
+def steps(offsets):
+    return sum(min(by, LENGTH[axis] - by) for axis, by in offsets)
+
+
 def rows(start, size):
     return pl.ds(start if isinstance(start, int) else pl.multiple_of(start, 8), size)
 
@@ -384,7 +388,7 @@
 def kernel(
     max_norm, count, slow, fast, momentum, slow_out, momentum_out, fast_out,
     slow_in, fast_in, momentum_in, diff, recv, total, squares, parts, factor,
-    load_sems, recv_sems, send_sems, norm_sems,
+    load_sems, recv_sems, send_sems, norm_sems, tokens,
 ):
     dp = lax.axis_index("dp")
     at = {"y": dp // 8, "z": lax.rem(dp // 2, 4), "x": lax.rem(dp, 2)}
@@ -447,15 +451,30 @@
     )
     events, _ = in_order(work.events + events)
 
-    friends += [moved(at, o) for o in others("yzx") if o[-1][0] == "x" and len(o) > 1]
+    near = [moved(at, ((axis, by),)) for axis in "yz" for by in (1, 3)]
+    partner = moved(at, (("x", 1),))
     barrier = pltpu.get_barrier_semaphore()
-    for device in friends:
+    for device in near + friends[-7:]:
         pl.semaphore_signal(barrier, inc=1, device_id=device, device_id_type=MESH)
-    pl.semaphore_wait(barrier, len(friends))
-
+    pl.semaphore_wait(barrier, len(near) + 7)
+
+    def tell(i):
+        for device in near + [partner]:
+            pl.semaphore_signal(tokens.at[i], inc=1, device_id=device, device_id_type=MESH)
+
+    def hear(i):
+        pl.semaphore_wait(tokens.at[i], len(near) + 1)
+
+    tell(0)
+    distant = [any(steps(hops) > 1 for _, _, hops in event.sends) for event in events].index(True)
     for i, event in enumerate(events):
         if i == len(CHUNKS):
             late.start()
+        if i == min(len(CHUNKS) + 2, distant):
+            hear(0)
+            tell(1)
+        if i == distant:
+            hear(1)
         event.run()
     exchange.drain(0)
     exchange.drain(1)
@@ -486,6 +505,7 @@
             pltpu.SemaphoreType.DMA((groups,)),
             pltpu.SemaphoreType.DMA((3,)),
             pltpu.SemaphoreType.DMA((2,)),
+            pltpu.SemaphoreType.REGULAR((2,)),
         ],
         compiler_params=pltpu.CompilerParams(
             collective_id=0, has_side_effects=True, vmem_limit_bytes=40 * 1024 * 1024

time: 53.9 us -> 53.2 us (0.987)
  Pallas kernels: 53.1 us -> 52 us
    pallas_call x1, Pallas kernels: 49.4 us -> 48.3 us  [updated(): pl.pallas_call(lambda *refs: kernel(max_norm, count, *refs), out_shape=(p...]
where the time goes in v5:
time: 53.2 us; the launch traced here: 52.6 us
  Pallas kernels  52 us (98%)
  between operations  0.64 us (1%)
    pallas_call x1, Pallas kernels, updated(): pl.pallas_call(lambda *refs: kernel(max_norm, count, *refs), out_shape=(p...  48.3 us
    pallas_call x1, Pallas kernels, written(): pl.pallas_call(run, out_shape=tuple((pltpu.HBM(x.shape, x.dtype) for x in...  3.67 us

profile of v5, /device:TPU:0, one launch (start us, length us, event | category | flops | bytes accessed | tf_op | source)
XLA Modules:
  0.0 52.6 jit_solution(16316040876419053069)
XLA Ops:
  0.6 48.3 %updated.1 = (f32[3584,256]{1,0:T(8,128)S(1)}, f32[3584,256]{1,0:T(8,128)S(1)}, bf16[3584,256]{1,0:T(8,128)(2,1)S(1)}) custom-call(f32[3584,256]{1,0:T(8,128)} %bitcast.6, bf16[3584,256]{1,0:T(8,128)(2,1)} %bitcast.8, f32[3584,256]{1,0:T(8,128)} %bitcast.7), custom_call_target="tpu_custom_call" | custom-call | tf_op jit(solution)/shard_map/updated/pallas_call | solution.py:489
  49.0 3.7 %written.1 = (f32[3584,256]{1,0:T(8,128)}, f32[3584,256]{1,0:T(8,128)}, bf16[3584,256]{1,0:T(8,128)(2,1)}) custom-call(f32[3584,256]{1,0:T(8,128)S(1)} %get-tuple-element.9.refs_0_, f32[3584,256]{1,0:T(8,128)S(1)} %get-tuple-element.10.refs_1_, bf16[3584,256]{1,0:T(8,128)(2,1)S(1)} %get-tuple-element.11.refs_2_), custom_call_target="tpu_custom_call" | custom-call | tf_op jit(solution)/shard_map/written/pallas_call | solution.py:526

commit v6 on v5

--- a/solution.py
+++ b/solution.py
@@ -16,8 +16,24 @@
 LENGTH = {"x": 2, "y": 4, "z": 4}
 COLUMNS = 256
 Y, Z = ("r:y", "d:zx"), ("r:z", "d:yx")
-XY, XZ = ("d:x", "r:y", "d:z"), ("d:x", "r:z", "d:y")
-CHUNKS = ((('r:z', 'd:x', 'd:y'), 256, False, ((-3, 3.8), (-2, 21.5), (-1, 5.5))), (('r:y', 'd:zx'), 256, True, ((-3, 0), (-1, 24.3), (0, 2.4))), (('r:y', 'd:x', 'd:z'), 256, False, ((-3, 7.3), (-2, 20.8), (-1, 24.4), (1, 2.7))), (('r:z', 'd:x', 'd:y'), 256, False, ((-3, 17.4), (-2, 11.1), (-1, 16.4), (1, 1.7))), (('r:y', 'd:zx'), 256, True, ((-3, 25.2), (-2, 3.6), (-1, 14.7), (1, 9.6))), (('d:x', 'r:z', 'd:y'), 256, False, ((-3, 1.7), (-1, 14.7), (1, 1.0))), (('r:y', 'd:zx'), 256, False, ((-3, 21.7), (-2, 18.7), (-1, 15.2), (1, 10.1))), (('r:z', 'd:x', 'd:y'), 256, True, ((-3, 20.1), (-2, 0), (-1, 5.5))), (('r:z', 'd:yx'), 256, True, ((-2, 12.5), (-1, 13.4), (0, 1.3), (1, 14.0))), (('d:x', 'd:y', 'd:z'), 256, True, ((-3, 5.6), (-1, 13.5), (0, 3.2), (1, 0.2))), (('r:y', 'd:zx'), 256, True, ((-2, 10.2), (-1, 4.9), (0, 5.1), (1, 11.6))), (('r:y', 'd:zx'), 256, True, ((-2, 0), (-1, 12.0))), (('r:z', 'd:x', 'd:y'), 256, True, ((-1, 20.7),)), (('d:x', 'd:z', 'd:y'), 256, False, ((-3, 5.2),)))
+YX, ZX = ("r:y", "d:x", "d:z"), ("r:z", "d:x", "d:y")
+XY, XZ = ("d:x", "d:y", "d:z"), ("d:x", "d:z", "d:y")
+CHUNKS = (
+    (Z, 256, True, ((-2, 6.0), (-1, 20.8),)),
+    (Z, 256, False, ((-3, 18.1), (-2, 13.7), (-1, 17.1), (0, 5.3),)),
+    (YX, 256, False, ((-1, 15.9),)),
+    (XY, 256, False, ((-2, 8.0), (1, 6.3),)),
+    (Z, 256, True, ((-1, 0), (0, 5.9),)),
+    (YX, 256, True, ((-3, 10.1), (-2, 10.1), (-1, 17.2),)),
+    (YX, 256, True, ((-1, 9.3), (1, 0),)),
+    (Z, 256, False, ((-2, 0), (-1, 20.7), (0, 7.7), (1, 14.2),)),
+    (Z, 256, True, ((-3, 8.6), (-1, 2.6),)),
+    (XY, 256, True, ((-3, 17.7), (-2, 23.0), (-1, 19.6), (1, 5.9),)),
+    (XY, 256, False, ((-3, 1.0), (-1, 6.8),)),
+    (YX, 256, False, ((-2, 6.4), (-1, 19.2),)),
+    (Z, 256, True, ((-1, 7.8), (0, 0),)),
+    (Z, 256, False, ((-3, 3.0), (1, 10.7),)),
+)
 LOADS = (512, 768, 1024, 1280)
 RATE = 45e3
 HOP = (2.7, 0.5)

time: 53.2 us -> 51.7 us (0.972)
  Pallas kernels: 52 us -> 51 us
    pallas_call x1, Pallas kernels: 48.3 us -> 47.3 us  [updated(): pl.pallas_call(lambda *refs: kernel(max_norm, count, *refs), out_shape=(p...]
where the time goes in v6:
time: 51.7 us; the launch traced here: 51.6 us
  Pallas kernels  51 us (99%)
  between operations  0.64 us (1%)
    pallas_call x1, Pallas kernels, updated(): pl.pallas_call(lambda *refs: kernel(max_norm, count, *refs), out_shape=(p...  47.3 us
    pallas_call x1, Pallas kernels, written(): pl.pallas_call(run, out_shape=tuple((pltpu.HBM(x.shape, x.dtype) for x in...  3.67 us

profile of v6, /device:TPU:0, one launch (start us, length us, event | category | flops | bytes accessed | tf_op | source)
XLA Modules:
  0.0 51.6 jit_solution(16418871128350333826)
XLA Ops:
  0.6 47.3 %updated.1 = (f32[3584,256]{1,0:T(8,128)S(1)}, f32[3584,256]{1,0:T(8,128)S(1)}, bf16[3584,256]{1,0:T(8,128)(2,1)S(1)}) custom-call(f32[3584,256]{1,0:T(8,128)} %bitcast.6, bf16[3584,256]{1,0:T(8,128)(2,1)} %bitcast.8, f32[3584,256]{1,0:T(8,128)} %bitcast.7), custom_call_target="tpu_custom_call" | custom-call | tf_op jit(solution)/shard_map/updated/pallas_call | solution.py:505
  47.9 3.7 %written.1 = (f32[3584,256]{1,0:T(8,128)}, f32[3584,256]{1,0:T(8,128)}, bf16[3584,256]{1,0:T(8,128)(2,1)}) custom-call(f32[3584,256]{1,0:T(8,128)S(1)} %get-tuple-element.9.refs_0_, f32[3584,256]{1,0:T(8,128)S(1)} %get-tuple-element.10.refs_1_, bf16[3584,256]{1,0:T(8,128)(2,1)S(1)} %get-tuple-element.11.refs_2_), custom_call_target="tpu_custom_call" | custom-call | tf_op jit(solution)/shard_map/written/pallas_call | solution.py:542

commit v7 on v6

--- a/solution.py
+++ b/solution.py
@@ -20,15 +20,15 @@
 XY, XZ = ("d:x", "d:y", "d:z"), ("d:x", "d:z", "d:y")
 CHUNKS = (
     (Z, 256, True, ((-2, 6.0), (-1, 20.8),)),
+    (Z, 256, True, ((-1, 0), (0, 5.9),)),
+    (YX, 256, False, ((-1, 15.9),)),
+    (Z, 256, False, ((-2, 0), (-1, 20.7), (0, 7.7), (1, 14.2),)),
+    (XY, 256, True, ((-3, 17.7), (-2, 23.0), (-1, 18.3), (1, 5.9),)),
+    (YX, 256, True, ((-3, 10.1), (-2, 10.1), (-1, 17.2),)),
     (Z, 256, False, ((-3, 18.1), (-2, 13.7), (-1, 17.1), (0, 5.3),)),
-    (YX, 256, False, ((-1, 15.9),)),
-    (XY, 256, False, ((-2, 8.0), (1, 6.3),)),
-    (Z, 256, True, ((-1, 0), (0, 5.9),)),
-    (YX, 256, True, ((-3, 10.1), (-2, 10.1), (-1, 17.2),)),
-    (YX, 256, True, ((-1, 9.3), (1, 0),)),
-    (Z, 256, False, ((-2, 0), (-1, 20.7), (0, 7.7), (1, 14.2),)),
+    (YX, 256, True, ((-3, 22.2), (-1, 9.3), (1, 0),)),
     (Z, 256, True, ((-3, 8.6), (-1, 2.6),)),
-    (XY, 256, True, ((-3, 17.7), (-2, 23.0), (-1, 19.6), (1, 5.9),)),
+    (XY, 256, False, ((-3, 0), (-2, 8.0), (1, 6.3),)),
     (XY, 256, False, ((-3, 1.0), (-1, 6.8),)),
     (YX, 256, False, ((-2, 6.4), (-1, 19.2),)),
     (Z, 256, True, ((-1, 7.8), (0, 0),)),

time: 51.7 us -> 51.7 us (level)
  no operation moved by 1% of the time
where the time goes in v7:
time: 51.7 us; the launch traced here: 51.6 us
  Pallas kernels  51 us (99%)
  between operations  0.64 us (1%)
    pallas_call x1, Pallas kernels, updated(): pl.pallas_call(lambda *refs: kernel(max_norm, count, *refs), out_shape=(p...  47.3 us
    pallas_call x1, Pallas kernels, written(): pl.pallas_call(run, out_shape=tuple((pltpu.HBM(x.shape, x.dtype) for x in...  3.67 us

profile of v7, /device:TPU:0, one launch (start us, length us, event | category | flops | bytes accessed | tf_op | source)
XLA Modules:
  0.0 51.6 jit_solution(8460385262864835240)
XLA Ops:
  0.6 47.3 %updated.1 = (f32[3584,256]{1,0:T(8,128)S(1)}, f32[3584,256]{1,0:T(8,128)S(1)}, bf16[3584,256]{1,0:T(8,128)(2,1)S(1)}) custom-call(f32[3584,256]{1,0:T(8,128)} %bitcast.6, bf16[3584,256]{1,0:T(8,128)(2,1)} %bitcast.8, f32[3584,256]{1,0:T(8,128)} %bitcast.7), custom_call_target="tpu_custom_call" | custom-call | tf_op jit(solution)/shard_map/updated/pallas_call | solution.py:505
  48.0 3.7 %written.1 = (f32[3584,256]{1,0:T(8,128)}, f32[3584,256]{1,0:T(8,128)}, bf16[3584,256]{1,0:T(8,128)(2,1)}) custom-call(f32[3584,256]{1,0:T(8,128)S(1)} %get-tuple-element.9.refs_0_, f32[3584,256]{1,0:T(8,128)S(1)} %get-tuple-element.10.refs_1_, bf16[3584,256]{1,0:T(8,128)(2,1)S(1)} %get-tuple-element.11.refs_2_), custom_call_target="tpu_custom_call" | custom-call | tf_op jit(solution)/shard_map/written/pallas_call | solution.py:542
